TPU v7x, 8 devices: a whole 2x2x1 slice. The times are simulated.
8 devices in a mesh: ens: 1 (over z), col: 2 (over y), row: 4 (over x, core).
Axes of the slice: x: 2, y: 2, z: 1, core: 2. Of those that a mesh axis runs over, the one named last changes fastest.
Arguments:
- u_init: float32 [2048, 2048], P(('ens', 'row'), 'col')
- v_init: float32 [2048, 2048], P(('ens', 'row'), 'col')
- stencil_w: float32 [64, 3, 3], replicated
Outputs:
- output 1: float32 [2048, 2048], P(('ens', 'row'), 'col')
- output 2: float32 [2048, 2048], P(('ens', 'row'), 'col')
All inputs are finite; a program needn't handle non-finite values.
Results may differ from a plain program's by a relative error of at most 0.001.
Values are sent between devices in bfloat16 or wider.
A program may use at most 1 GiB of HBM per device.

v0:
```python
import jax
import jax.numpy as jnp
from jax import lax
from jax.sharding import PartitionSpec as P

TIME_STEP = 0.5


def stencil_valid(block, step_w):
    out_rows = block.shape[0] - 2
    out_cols = block.shape[1] - 2
    total_acc = step_w[0, 0] * block[0:out_rows, 0:out_cols]
    for tap_index in range(1, 9):
        row_off, col_off = divmod(tap_index, 3)
        total_acc = total_acc + step_w[row_off, col_off] * block[row_off:row_off + out_rows, col_off:col_off + out_cols]
    return total_acc


def solution(mesh):
    row_devices = mesh.shape["row"]
    col_devices = mesh.shape["col"]
    row_fwd = [(source_dev, (source_dev + 1) % row_devices) for source_dev in range(row_devices)]
    row_back = [(source_dev, (source_dev - 1) % row_devices) for source_dev in range(row_devices)]
    col_fwd = [(source_dev, (source_dev + 1) % col_devices) for source_dev in range(col_devices)]
    col_back = [(source_dev, (source_dev - 1) % col_devices) for source_dev in range(col_devices)]
    tile_spec = P(("ens", "row"), "col")

    def halo_pad(u_tile):
        from_above = lax.ppermute(u_tile[-1:, :], "row", row_fwd)
        from_below = lax.ppermute(u_tile[:1, :], "row", row_back)
        tall_tile = jnp.concatenate([from_above, u_tile, from_below], axis=0)
        from_left = lax.ppermute(tall_tile[:, -1:], "col", col_fwd)
        from_right = lax.ppermute(tall_tile[:, :1], "col", col_back)
        return jnp.concatenate([from_left, tall_tile, from_right], axis=1)

    def local_run(u_tile, v_tile, stencil_w):
        def one_step(state_pair, step_w):
            u_now, v_now = state_pair
            padded = halo_pad(u_now)
            v_next = v_now + (stencil_valid(padded, step_w) - u_now)
            u_next = u_now + TIME_STEP * v_next
            return (u_next, v_next), None

        (u_final, v_final), _ = lax.scan(one_step, (u_tile, v_tile), stencil_w)
        return u_final, v_final

    return jax.shard_map(local_run, mesh=mesh, in_specs=(tile_spec, tile_spec, P()), out_specs=(tile_spec, tile_spec), check_vma=False)
```

profile of v0, /device:TPU:0, one launch (start us, length us, event | category | flops | bytes accessed | tf_op | source)
XLA Modules:
  0.0 1998.1 jit_solution(4004241757475492916)
XLA Ops:
  5.4 1992.6 %while.12 = (s32[]{:T(128)}, f32[512,1024]{1,0:T(8,128)}, f32[512,1024]{1,0:T(8,128)}, f32[64,3,3]{2,1,0:T(4,128)S(1)}, s32[]{:T(128)}) while((s32[]{:T(128)}, f32[512,1024]{1,0:T(8,128)}, f32[512,1024]{1,0:T(8,128)}, f32[64,3,3]{2,1,0:T(4,128)S(1)}, s32[]{:T(128)}) %tuple.45), condition=%wide.region_1.2_spmd, body=%wide.region_0.1_spmd.sunk | while | flops 15221782 | bytes 50451004 | solution.py:44
  89.6 10.7 multiply_add_fusion.2
  151.8 10.7 multiply_add_fusion.2
  214.0 10.7 multiply_add_fusion.2
  431.7 10.7 multiply_add_fusion.2
  493.9 10.7 multiply_add_fusion.2
  556.1 10.7 multiply_add_fusion.2
  649.2 10.7 multiply_add_fusion.2
  711.4 10.7 multiply_add_fusion.2
  773.5 10.7 multiply_add_fusion.2
  991.3 10.7 multiply_add_fusion.2
  1053.5 10.7 multiply_add_fusion.2
  1115.6 10.7 multiply_add_fusion.2
  1177.8 10.7 multiply_add_fusion.2
  1208.8 10.7 multiply_add_fusion.2
  1270.9 10.7 multiply_add_fusion.2
  1333.1 10.7 multiply_add_fusion.2
  1395.3 10.7 multiply_add_fusion.2
  1613.0 10.7 multiply_add_fusion.2
  1675.2 10.7 multiply_add_fusion.2
  1737.4 10.7 multiply_add_fusion.2
  1830.5 10.7 multiply_add_fusion.2
  1892.7 10.7 multiply_add_fusion.2
  1954.8 10.7 multiply_add_fusion.2
  (1200 shorter events, 1749.6 us)
Async XLA Ops:
  45.8 12.0 collective-permute-start.3
  108.0 12.0 collective-permute-start.3
  170.2 12.0 collective-permute-start.3
  232.3 12.0 collective-permute-start.3
  294.5 12.0 collective-permute-start.3
  356.7 12.0 collective-permute-start.3
  418.9 12.0 collective-permute-start.3
  481.0 12.0 collective-permute-start.3
  543.2 12.0 collective-permute-start.3
  605.4 12.0 collective-permute-start.3
  667.6 12.0 collective-permute-start.3
  729.7 12.0 collective-permute-start.3
  791.9 12.0 collective-permute-start.3
  854.1 12.0 collective-permute-start.3
  916.3 12.0 collective-permute-start.3
  978.4 12.0 collective-permute-start.3
  1040.6 12.0 collective-permute-start.3
  1102.8 12.0 collective-permute-start.3
  1164.9 12.0 collective-permute-start.3
  1227.1 12.0 collective-permute-start.3
  1289.3 12.0 collective-permute-start.3
  1351.5 12.0 collective-permute-start.3
  1413.6 12.0 collective-permute-start.3
  1973.2 12.0 collective-permute-start.3
  (362 other events, 2176.6 us)
where the time goes:
time: 2010 us; the launch traced here: 2000 us
  waiting for transfers between devices  846 us (42%)
  other arithmetic  747 us (37%)
  local copies, waits for them, and re-layouts  235 us (12%)
  starting transfers between devices  167 us (8%)
    add x64, other arithmetic, one_step(): u_next = u_now + TIME_STEP * v_next  683 us
    ppermute x64, waiting for transfers between devices, halo_pad(): from_left = lax.ppermute(tall_tile[:, -1:], 'col', col_fwd)  420 us
    ppermute x64, waiting for transfers between devices, halo_pad(): from_right = lax.ppermute(tall_tile[:, :1], 'col', col_back)  262 us
    while x320, local copies, waits for them, and re-layouts  186 us
    ppermute x64, waiting for transfers between devices, halo_pad(): from_above = lax.ppermute(u_tile[-1:, :], 'row', row_fwd)  111 us
    ppermute x64, starting transfers between devices, halo_pad(): from_left = lax.ppermute(tall_tile[:, -1:], 'col', col_fwd)  98.6 us
    concatenate x64, other arithmetic, halo_pad(): return jnp.concatenate([from_left, tall_tile, from_right], axis=1)  55.4 us
    ppermute x64, waiting for transfers between devices, halo_pad(): from_below = lax.ppermute(u_tile[:1, :], 'row', row_back)  53.6 us
  transfers between devices with their start and end apart: 256, of which 256 were waited for; matrix products, arithmetic and copies ran while one was open for 2% of the time, Pallas kernels for 0%

commit v1 on v0

v1 whole, which is shorter than its diff:
```python
import functools

import jax
import jax.numpy as jnp
from jax import lax
from jax.experimental import pallas as pl
from jax.experimental.pallas import tpu as pltpu
from jax.sharding import PartitionSpec as P

HALO = 16
CHUNK = 13
NC = 9
NB = 11
SCALE = 0.125
MESH = pl.DeviceIdType.MESH


def kernel(steps, rows, cols, halo, chunk, w_ref, u_hbm, v_hbm, uo_hbm, vo_hbm,
           raw, gsend, state_a, state_b, wide, edge, sbuf, rbuf,
           load_sem, col_sems, row_sems, diag_sems, send_sems, recv_sems, out_sem):
    R = (rows + 2 * halo) // 8
    nblk = cols // 128
    n_row = lax.axis_size("row")
    me_row, me_col = lax.axis_index("row"), lax.axis_index("col")
    up, down = lax.rem(me_row + n_row - 1, n_row), lax.rem(me_row + 1, n_row)
    other = 1 - me_col

    loads = []
    for f, src in enumerate((u_hbm, v_hbm)):
        for b in (0, nblk - 1, *range(1, nblk - 1)):
            cp = pltpu.make_async_copy(src.at[:, pl.ds(b * 128, 128)],
                                       raw.at[f, b, pl.ds(halo, rows), :], load_sem.at[f, b])
            cp.start()
            loads.append(cp)

    barrier = pltpu.get_barrier_semaphore()
    peers = [(up, me_col), (down, me_col), (me_row, other), (up, other), (down, other)]
    for r, c in peers:
        pl.semaphore_signal(barrier, inc=1, device_id={"row": r, "col": c}, device_id_type=MESH)
    pl.semaphore_wait(barrier, len(peers))

    states = (state_a, state_b)
    lane = lax.broadcasted_iota(jnp.int32, (8, 128), 1)

    def remote(src, dst, sems, r, c):
        cp = pltpu.make_async_remote_copy(src_ref=src, dst_ref=dst, send_sem=sems.at[0], recv_sem=sems.at[1],
                                          device_id={"row": r, "col": c}, device_id_type=MESH)
        cp.start()
        return cp

    first = [[], []]
    for f in range(2):
        mine = loads[f * nblk:(f + 1) * nblk]
        mine[0].wait()
        mine[1].wait()

        def build(i, _, f=f):
            for q in range(8):
                at = pl.multiple_of(i * 64 + q * 8, 8)
                gsend[f, pl.ds(at, 8), :] = jnp.where(lane < 64, raw[f, 0, pl.ds(halo + at, 8), :],
                                                      raw[f, nblk - 1, pl.ds(halo + at, 8), :])
            return 0
        lax.fori_loop(0, rows // 64, build, 0)
        first[f].append(remote(gsend.at[f], raw.at[f, nblk, pl.ds(halo, rows), :], col_sems.at[f], me_row, other))
        first[f].append(remote(gsend.at[f, pl.ds(0, halo), :], raw.at[f, nblk, pl.ds(halo + rows, halo), :],
                               diag_sems.at[f, 0], up, other))
        first[f].append(remote(gsend.at[f, pl.ds(rows - halo, halo), :], raw.at[f, nblk, pl.ds(0, halo), :],
                               diag_sems.at[f, 1], down, other))
        for cp in mine[2:]:
            cp.wait()
        first[f].append(remote(raw.at[f, pl.ds(0, nblk), pl.ds(halo, halo), :],
                               raw.at[f, pl.ds(0, nblk), pl.ds(halo + rows, halo), :], row_sems.at[f, 0], up, me_col))
        first[f].append(remote(raw.at[f, pl.ds(0, nblk), pl.ds(rows, halo), :],
                               raw.at[f, pl.ds(0, nblk), pl.ds(0, halo), :], row_sems.at[f, 1], down, me_col))

    groups = -(-R // 16)

    def reg(r, c):
        return pl.ds(pl.multiple_of((r * NB + c) * 8, 8), 8)

    for f in range(2):
        for cp in first[f]:
            cp.wait()

        def group(i, _, f=f):
            r0 = i * (R - 16) // (groups - 1)
            for b in range(NC):
                parts = []
                for q in range(16):
                    x = raw[0, b, pl.ds(r0 + q, 8, stride=R), :]
                    if f == 1:
                        x = x - 0.5 * raw[1, b, pl.ds(r0 + q, 8, stride=R), :]
                    parts.append(x * SCALE)
                wide[pl.ds(b * 128, 128), :] = jnp.concatenate(parts, axis=0).T
            for c in range(NC):
                back = wide[pl.ds(c, 128, stride=NC), :].T
                for q in range(16):
                    x = back[q * 8:q * 8 + 8, :]
                    states[f][reg(r0 + q, c), :] = x
                    if c == 0:
                        states[f][reg(r0 + q, 10), :] = pltpu.roll(x, 127, 1)
                    if c == NC - 1:
                        states[f][reg(r0 + q, 9), :] = pltpu.roll(x, 1, 1)
            return 0
        lax.fori_loop(0, groups, group, 0)

    def level(t, cur, new):
        w00, w01, w02, w10, w11 = (w_ref[t, 0, 0], w_ref[t, 0, 1], w_ref[t, 0, 2], w_ref[t, 1, 0], w_ref[t, 1, 1])
        splat = lambda x: jnp.full((8, 128), x, jnp.float32)
        alpha, beta = splat(0.25 * (w00 + w02)), splat(0.25 * (w02 - w00))
        side, mid_s, centre = splat(0.5 * w01), splat(0.5 * w10), splat(1.5 + 0.5 * w11)

        def contrib(r, want="TMB"):
            u = [cur[reg(r, c), :] for c in range(NB)]
            above, mid, below = [], [], []
            for c in range(NC):
                left = u[c - 1] if c else u[9]
                right = u[c + 1] if c < NC - 1 else u[10]
                s, d = left + right, right - left
                e, bd = alpha * s + side * u[c], beta * d
                above.append(e + bd)
                if "M" in want:
                    mid.append(mid_s * s + centre * u[c])
                    below.append(e - bd)
            return above, mid, below

        def emit(r, acc, below):
            for c in range(NC):
                x = (acc[c] + below[c]) - new[reg(r, c), :]
                new[reg(r, c), :] = x
                if c == 0:
                    new[reg(r, 10), :] = pltpu.roll(x, 127, 1)
                if c == NC - 1:
                    new[reg(r, 9), :] = pltpu.roll(x, 1, 1)

        last, _, _ = contrib(R - 1, "T")
        above, mid, below = contrib(0)
        for c in range(NC):
            edge[c] = pltpu.roll(below[c], 7, 0)
        acc = [pltpu.roll(last[c], 1, 0) + mid[c] for c in range(NC)]

        def rowstep(r, above, acc):
            nabove, mid, below = contrib(r + 1)
            emit(r, acc, below)
            return nabove, [above[c] + mid[c] for c in range(NC)]

        def body(it, carry):
            above, acc = carry
            for q in range(chunk):
                above, acc = rowstep(it * chunk + q, above, acc)
            return above, acc

        trips = (R - 1) // chunk
        above, acc = lax.fori_loop(0, trips, body, (above, acc))
        for r in range(trips * chunk, R - 1):
            above, acc = rowstep(r, above, acc)
        emit(R - 1, acc, [edge[c] for c in range(NC)])

    def pair(i, _):
        level(2 * i, state_a, state_b)
        level(2 * i + 1, state_b, state_a)
        return 0

    def strided(r, c, s):
        return pl.ds((r * NB + c) * 8 + s, 8, stride=NB * 8)

    def exchange(slot):
        copies = []
        for d, (peer, r0, s) in enumerate(((up, halo, 0), (down, R - 2 * halo, 7))):
            for f in range(2):
                for g in range(halo // 8):
                    for c in range(NB):
                        sbuf[slot, d, f, g, c] = states[f][strided(r0 + 8 * g, c, s), :]
            copies.append(pltpu.make_async_remote_copy(
                src_ref=sbuf.at[slot, d], dst_ref=rbuf.at[slot, d], send_sem=send_sems.at[slot, d],
                recv_sem=recv_sems.at[slot, d], device_id={"row": peer, "col": me_col}, device_id_type=MESH))
            copies[-1].start()
        for d, (r0, s) in enumerate(((R - halo, 7), (0, 0))):
            copies[d].wait()
            for f in range(2):
                for g in range(halo // 8):
                    for c in range(NB):
                        states[f][strided(r0 + 8 * g, c, s), :] = rbuf[slot, d, f, g, c]

    def phase(p, _):
        lax.fori_loop(p * (halo // 2), (p + 1) * (halo // 2), pair, 0)

        @pl.when(p < steps // halo - 1)
        def _():
            exchange(lax.rem(p, 2))
        return 0
    lax.fori_loop(0, steps // halo, phase, 0)

    outs = []
    for f, dst in enumerate((uo_hbm, vo_hbm)):
        def ungroup(i, _, f=f):
            r0 = i * (R - 16) // (groups - 1)
            for c in range(NC):
                parts = []
                for q in range(16):
                    x = state_a[reg(r0 + q, c), :]
                    if f == 1:
                        x = (x - state_b[reg(r0 + q, c), :]) * (2.0 / SCALE)
                    else:
                        x = x * (1.0 / SCALE)
                    parts.append(x)
                wide[pl.ds(c, 128, stride=NC), :] = jnp.concatenate(parts, axis=0).T
            for b in range(nblk):
                back = wide[pl.ds(b * 128, 128), :].T
                for q in range(16):
                    raw[f, b, pl.ds(r0 + q, 8, stride=R), :] = back[q * 8:q * 8 + 8, :]
            return 0
        lax.fori_loop(0, groups, ungroup, 0)
        for b in range(nblk):
            cp = pltpu.make_async_copy(raw.at[f, b, pl.ds(halo, rows), :], dst.at[:, pl.ds(b * 128, 128)],
                                       out_sem.at[f, b])
            cp.start()
            outs.append(cp)
    for cp in outs:
        cp.wait()


def solution(mesh):
    tile_spec = P(("ens", "row"), "col")

    def local_run(u_tile, v_tile, stencil_w):
        rows, cols = u_tile.shape
        steps = stencil_w.shape[0]
        halo = HALO
        R = (rows + 2 * halo) // 8
        nblk = cols // 128
        f32 = jnp.float32
        dma = pltpu.SemaphoreType.DMA
        return pl.pallas_call(
            functools.partial(kernel, steps, rows, cols, halo, CHUNK),
            out_shape=[jax.ShapeDtypeStruct((rows, cols), f32)] * 2,
            in_specs=[pl.BlockSpec(memory_space=pltpu.SMEM)] + [pl.BlockSpec(memory_space=pl.ANY)] * 2,
            out_specs=[pl.BlockSpec(memory_space=pl.ANY)] * 2,
            scratch_shapes=[
                pltpu.VMEM((2, nblk + 1, 8 * R, 128), f32),
                pltpu.VMEM((2, rows, 128), f32),
                pltpu.VMEM((R * NB * 8, 128), f32),
                pltpu.VMEM((R * NB * 8, 128), f32),
                pltpu.VMEM((128 * NC, 128), f32),
                pltpu.VMEM((NC, 8, 128), f32),
                pltpu.VMEM((2, 2, 2, halo // 8, NB, 8, 128), f32),
                pltpu.VMEM((2, 2, 2, halo // 8, NB, 8, 128), f32),
                dma((2, nblk)), dma((2, 2)), dma((2, 2, 2)), dma((2, 2, 2)), dma((2, 2)), dma((2, 2)), dma((2, nblk)),
            ],
            compiler_params=pltpu.CompilerParams(collective_id=0, has_side_effects=True,
                                                 vmem_limit_bytes=48 * 1024 * 1024),
        )(stencil_w, u_tile, v_tile)

    return jax.shard_map(local_run, mesh=mesh, in_specs=(tile_spec, tile_spec, P()), out_specs=(tile_spec, tile_spec), check_vma=False)
```

time: 2010 us -> 150 us (0.07)
  waiting for transfers between devices: 846 us -> 0 us
  other arithmetic: 747 us -> 0 us
  local copies, waits for them, and re-layouts: 235 us -> 3.45 us
  starting transfers between devices: 167 us -> 0 us
  Pallas kernels: 0 us -> 146 us
    ppermute x256 -> x0, waiting for transfers between devices: 846 us -> none  [the longest x64 420 us: halo_pad(): from_left = lax.ppermute(tall_tile[:, -1:], 'col', col_fwd)]
    add x64 -> x0, other arithmetic: 683 us -> none  [one_step(): u_next = u_now + TIME_STEP * v_next]
    while x321 -> x0, local copies, waits for them, and re-layouts: 187 us -> none
    ppermute x256 -> x0, starting transfers between devices: 167 us -> none  [the longest x64 98.6 us: halo_pad(): from_left = lax.ppermute(tall_tile[:, -1:], 'col', col_fwd)]
    pallas_call x0 -> x1, Pallas kernels: none -> 146 us  [local_run(): pl.pallas_call(functools.partial(kernel, steps, rows, cols, halo, CHUNK),...]
    concatenate x64 -> x0, other arithmetic: 55.4 us -> none  [halo_pad(): return jnp.concatenate([from_left, tall_tile, from_right], axis=1)]
    slice x128 -> x0, local copies, waits for them, and re-layouts: 43.8 us -> none  [the longest x64 43.4 us: stencil_valid(): total_acc = step_w[0, 0] * block[0:out_rows, 0:out_cols]]
  transfers between devices with their start and end apart: 256 -> 0, of which waited for: 256 -> 0; matrix products, arithmetic and copies ran while one was open for 2% -> 0% of each run, Pallas kernels for 0% -> 0%
where the time goes in v1:
time: 150 us
  Pallas kernels  146 us (97%)
  local copies, waits for them, and re-layouts  3.45 us (2%)
    pallas_call x1, Pallas kernels, local_run(): pl.pallas_call(functools.partial(kernel, steps, rows, cols, halo, CHUNK),...  146 us
    unnamed x3, local copies, waits for them, and re-layouts  3.45 us

profile of v1, /device:TPU:0, one launch (start us, length us, event | category | flops | bytes accessed | tf_op | source)
XLA Modules:
  0.0 150.1 jit_solution(5795893472937295924)
XLA Ops:
  0.6 0.8 copy.5.w_ref
  1.5 146.0 %shard_map.50 = (f32[512,1024]{1,0:T(8,128)S(1)}, f32[512,1024]{1,0:T(8,128)S(1)}) custom-call(f32[64,3,3]{2,1,0:T(4,128)S(1)} %copy.5.w_ref, f32[512,1024]{1,0:T(8,128)} %u_hbm.1, f32[512,1024]{1,0:T(8,128)} %v_hbm.1), custom_call_target="tpu_custom_call" | custom-call | tf_op jit(solution)/shard_map/pallas_call | solution.py:234
  147.4 1.3 copy.8
  148.8 1.3 copy.9

commit v2 on v1

--- a/solution.py
+++ b/solution.py
@@ -8,7 +8,8 @@
 from jax.sharding import PartitionSpec as P
 
 HALO = 16
-CHUNK = 13
+CHUNK = 22
+ORDER = ((0, 8), (1, 2, 3, 4), (5, 6, 7))
 NC = 9
 NB = 11
 SCALE = 0.125
@@ -16,7 +17,7 @@
 
 
 def kernel(steps, rows, cols, halo, chunk, w_ref, u_hbm, v_hbm, uo_hbm, vo_hbm,
-           raw, gsend, state_a, state_b, wide, edge, sbuf, rbuf,
+           raw, gsend, state_a, state_b, wide, sbuf, rbuf,
            load_sem, col_sems, row_sems, diag_sems, send_sems, recv_sems, out_sem):
     R = (rows + 2 * halo) // 8
     nblk = cols // 128
@@ -110,86 +111,107 @@
         alpha, beta = splat(0.25 * (w00 + w02)), splat(0.25 * (w02 - w00))
         side, mid_s, centre = splat(0.5 * w01), splat(0.5 * w10), splat(1.5 + 0.5 * w11)
 
-        def contrib(r, want="TMB"):
-            u = [cur[reg(r, c), :] for c in range(NB)]
-            above, mid, below = [], [], []
-            for c in range(NC):
-                left = u[c - 1] if c else u[9]
-                right = u[c + 1] if c < NC - 1 else u[10]
-                s, d = left + right, right - left
-                e, bd = alpha * s + side * u[c], beta * d
-                above.append(e + bd)
-                if "M" in want:
-                    mid.append(mid_s * s + centre * u[c])
-                    below.append(e - bd)
-            return above, mid, below
-
-        def emit(r, acc, below):
-            for c in range(NC):
-                x = (acc[c] + below[c]) - new[reg(r, c), :]
-                new[reg(r, c), :] = x
-                if c == 0:
-                    new[reg(r, 10), :] = pltpu.roll(x, 127, 1)
-                if c == NC - 1:
-                    new[reg(r, 9), :] = pltpu.roll(x, 1, 1)
-
-        last, _, _ = contrib(R - 1, "T")
-        above, mid, below = contrib(0)
+        def contrib(r, c):
+            here = cur[reg(r, c), :]
+            left = cur[reg(r, c - 1 if c else 9), :]
+            right = cur[reg(r, c + 1 if c < NC - 1 else 10), :]
+            s, d = left + right, right - left
+            e, bd = alpha * s + side * here, beta * d
+            return e + bd, mid_s * s + centre * here, e - bd
+
+        def emit(r, c, acc, below):
+            x = (acc + below) - new[reg(r, c), :]
+            new[reg(r, c), :] = x
+            return x
+
+        def edges(r, c, x):
+            if c == 0:
+                new[reg(r, 10), :] = pltpu.roll(x, 127, 1)
+            if c == NC - 1:
+                new[reg(r, 9), :] = pltpu.roll(x, 1, 1)
+
+        lead = (R - 1) % chunk
+        carry = []
         for c in range(NC):
-            edge[c] = pltpu.roll(below[c], 7, 0)
-        acc = [pltpu.roll(last[c], 1, 0) + mid[c] for c in range(NC)]
-
-        def rowstep(r, above, acc):
-            nabove, mid, below = contrib(r + 1)
-            emit(r, acc, below)
-            return nabove, [above[c] + mid[c] for c in range(NC)]
+            before, _, _ = contrib(R - 2, c)
+            last, mid, _ = contrib(R - 1, c)
+            above, mid0, below = contrib(0, c)
+            emit(R - 1, c, before + mid, pltpu.roll(below, 7, 0))
+            acc = pltpu.roll(last, 1, 0) + mid0
+            for r in range(lead):
+                nabove, mid, below = contrib(r + 1, c)
+                emit(r, c, acc, below)
+                above, acc = nabove, above + mid
+            carry.append((above, acc))
 
         def body(it, carry):
-            above, acc = carry
-            for q in range(chunk):
-                above, acc = rowstep(it * chunk + q, above, acc)
-            return above, acc
-
-        trips = (R - 1) // chunk
-        above, acc = lax.fori_loop(0, trips, body, (above, acc))
-        for r in range(trips * chunk, R - 1):
-            above, acc = rowstep(r, above, acc)
-        emit(R - 1, acc, [edge[c] for c in range(NC)])
+            carry = list(carry)
+            for r in (R - 1, *range(lead)):
+                for c in (0, NC - 1):
+                    edges(r, c, new[reg(r, c), :])
+            for cs in ORDER:
+                for q in range(chunk):
+                    r = it * chunk + lead + q
+                    for c in cs:
+                        above, acc = carry[c]
+                        nabove, mid, below = contrib(r + 1, c)
+                        edges(r, c, emit(r, c, acc, below))
+                        carry[c] = nabove, above + mid
+            return tuple(carry)
+
+        lax.fori_loop(0, (R - 1) // chunk, body, tuple(carry))
+
+    def strided(r, c, s):
+        return pl.ds((r * NB + c) * 8 + s, 8, stride=NB * 8)
+
+    def copies(f, slot):
+        return [pltpu.make_async_remote_copy(
+            src_ref=sbuf.at[slot, d, f], dst_ref=rbuf.at[slot, d, f], send_sem=send_sems.at[slot, d, f],
+            recv_sem=recv_sems.at[slot, d, f], device_id={"row": peer, "col": me_col}, device_id_type=MESH)
+            for d, peer in enumerate((up, down))]
+
+    def send(f, slot):
+        for d, (r0, s) in enumerate(((halo, 0), (R - 2 * halo, 7))):
+            for g in range(halo // 8):
+                for c in range(NC):
+                    sbuf[slot, d, f, g, c] = states[f][strided(r0 + 8 * g, c, s), :]
+        for cp in copies(f, slot):
+            cp.start()
+
+    def receive(f, slot):
+        for d, (r0, s) in enumerate(((R - halo, 7), (0, 0))):
+            copies(f, slot)[d].wait()
+            for g in range(halo // 8):
+                for c in range(NC):
+                    states[f][strided(r0 + 8 * g, c, s), :] = rbuf[slot, d, f, g, c]
+
+        def fix(i, _):
+            for r0 in (0, R - halo):
+                for q in range(8):
+                    r = r0 + i * 8 + q
+                    states[f][reg(r, 10), :] = pltpu.roll(states[f][reg(r, 0), :], 127, 1)
+                    states[f][reg(r, 9), :] = pltpu.roll(states[f][reg(r, NC - 1), :], 1, 1)
+            return 0
+        lax.fori_loop(0, halo // 8, fix, 0)
 
     def pair(i, _):
         level(2 * i, state_a, state_b)
+        done = lax.rem(2 * i + 2, halo) == 0
+        more = 2 * i + 2 < steps
+        slot = lax.rem((2 * i + 2) // halo, 2)
+
+        @pl.when(done & more)
+        def _():
+            send(1, slot)
         level(2 * i + 1, state_b, state_a)
+
+        @pl.when(done & more)
+        def _():
+            send(0, slot)
+            receive(1, slot)
+            receive(0, slot)
         return 0
-
-    def strided(r, c, s):
-        return pl.ds((r * NB + c) * 8 + s, 8, stride=NB * 8)
-
-    def exchange(slot):
-        copies = []
-        for d, (peer, r0, s) in enumerate(((up, halo, 0), (down, R - 2 * halo, 7))):
-            for f in range(2):
-                for g in range(halo // 8):
-                    for c in range(NB):
-                        sbuf[slot, d, f, g, c] = states[f][strided(r0 + 8 * g, c, s), :]
-            copies.append(pltpu.make_async_remote_copy(
-                src_ref=sbuf.at[slot, d], dst_ref=rbuf.at[slot, d], send_sem=send_sems.at[slot, d],
-                recv_sem=recv_sems.at[slot, d], device_id={"row": peer, "col": me_col}, device_id_type=MESH))
-            copies[-1].start()
-        for d, (r0, s) in enumerate(((R - halo, 7), (0, 0))):
-            copies[d].wait()
-            for f in range(2):
-                for g in range(halo // 8):
-                    for c in range(NB):
-                        states[f][strided(r0 + 8 * g, c, s), :] = rbuf[slot, d, f, g, c]
-
-    def phase(p, _):
-        lax.fori_loop(p * (halo // 2), (p + 1) * (halo // 2), pair, 0)
-
-        @pl.when(p < steps // halo - 1)
-        def _():
-            exchange(lax.rem(p, 2))
-        return 0
-    lax.fori_loop(0, steps // halo, phase, 0)
+    lax.fori_loop(0, steps // 2, pair, 0)
 
     outs = []
     for f, dst in enumerate((uo_hbm, vo_hbm)):
@@ -242,10 +264,9 @@
                 pltpu.VMEM((R * NB * 8, 128), f32),
                 pltpu.VMEM((R * NB * 8, 128), f32),
                 pltpu.VMEM((128 * NC, 128), f32),
-                pltpu.VMEM((NC, 8, 128), f32),
-                pltpu.VMEM((2, 2, 2, halo // 8, NB, 8, 128), f32),
-                pltpu.VMEM((2, 2, 2, halo // 8, NB, 8, 128), f32),
-                dma((2, nblk)), dma((2, 2)), dma((2, 2, 2)), dma((2, 2, 2)), dma((2, 2)), dma((2, 2)), dma((2, nblk)),
+                pltpu.VMEM((2, 2, 2, halo // 8, NC, 8, 128), f32),
+                pltpu.VMEM((2, 2, 2, halo // 8, NC, 8, 128), f32),
+                dma((2, nblk)), dma((2, 2)), dma((2, 2, 2)), dma((2, 2, 2)), dma((2, 2, 2)), dma((2, 2, 2)), dma((2, nblk)),
             ],
             compiler_params=pltpu.CompilerParams(collective_id=0, has_side_effects=True,
                                                  vmem_limit_bytes=48 * 1024 * 1024),

time: 150 us -> 122 us (0.81)
  Pallas kernels: 146 us -> 118 us
    pallas_call x1, Pallas kernels: 146 us -> 118 us  [local_run(): pl.pallas_call(functools.partial(kernel, steps, rows, cols, halo, CHUNK),...]
where the time goes in v2:
time: 122 us
  Pallas kernels  118 us (97%)
  local copies, waits for them, and re-layouts  3.45 us (3%)
    pallas_call x1, Pallas kernels, local_run(): pl.pallas_call(functools.partial(kernel, steps, rows, cols, halo, CHUNK),...  118 us
    unnamed x3, local copies, waits for them, and re-layouts  3.45 us

profile of v2, /device:TPU:0, one launch (start us, length us, event | category | flops | bytes accessed | tf_op | source)
XLA Modules:
  0.0 122.0 jit_solution(9981884116597697390)
XLA Ops:
  0.6 0.8 copy.5.w_ref
  1.5 117.9 %shard_map.50 = (f32[512,1024]{1,0:T(8,128)S(1)}, f32[512,1024]{1,0:T(8,128)S(1)}) custom-call(f32[64,3,3]{2,1,0:T(4,128)S(1)} %copy.5.w_ref, f32[512,1024]{1,0:T(8,128)} %u_hbm.1, f32[512,1024]{1,0:T(8,128)} %v_hbm.1), custom_call_target="tpu_custom_call" | custom-call | tf_op jit(solution)/shard_map/pallas_call | solution.py:256
  119.3 1.3 %copy.8 = f32[512,1024]{1,0:T(8,128)} copy(f32[512,1024]{1,0:T(8,128)S(1)} %get-tuple-element.4) | data formatting | bytes 4194304
  120.6 1.3 %copy.9 = f32[512,1024]{1,0:T(8,128)} copy(f32[512,1024]{1,0:T(8,128)S(1)} %get-tuple-element.5) | data formatting | bytes 4194304

commit v3 on v2

v3 whole, which is shorter than its diff:
```python
import functools

import jax
import jax.numpy as jnp
from jax import lax
from jax.experimental import pallas as pl
from jax.experimental.pallas import tpu as pltpu
from jax.sharding import PartitionSpec as P

HALO = 16
PARTS = 2
NC = 9
NB = 11
SCALE = 0.125
MESH = pl.DeviceIdType.MESH


def kernel(steps, rows, cols, halo, w_ref, u_hbm, v_hbm, uo_hbm, vo_hbm,
           raw, gsend, state_a, state_b, coef, wide, sbuf, rbuf,
           load_sem, col_sems, row_sems, diag_sems, send_sems, recv_sems, out_sem):
    R = (rows + 2 * halo) // 8
    nblk = cols // 128
    n_row = lax.axis_size("row")
    me_row, me_col = lax.axis_index("row"), lax.axis_index("col")
    up, down = lax.rem(me_row + n_row - 1, n_row), lax.rem(me_row + 1, n_row)
    other = 1 - me_col

    loads = []
    for f, src in enumerate((u_hbm, v_hbm)):
        for b in (0, nblk - 1, *range(1, nblk - 1)):
            cp = pltpu.make_async_copy(src.at[:, pl.ds(b * 128, 128)],
                                       raw.at[f, b, pl.ds(halo, rows), :], load_sem.at[f, b])
            cp.start()
            loads.append(cp)

    barrier = pltpu.get_barrier_semaphore()
    peers = [(up, me_col), (down, me_col), (me_row, other), (up, other), (down, other)]
    for r, c in peers:
        pl.semaphore_signal(barrier, inc=1, device_id={"row": r, "col": c}, device_id_type=MESH)
    pl.semaphore_wait(barrier, len(peers))

    states = (state_a, state_b)
    lane = lax.broadcasted_iota(jnp.int32, (8, 128), 1)

    def remote(src, dst, sems, r, c):
        cp = pltpu.make_async_remote_copy(src_ref=src, dst_ref=dst, send_sem=sems.at[0], recv_sem=sems.at[1],
                                          device_id={"row": r, "col": c}, device_id_type=MESH)
        cp.start()
        return cp

    halos = []
    for f in range(2):
        mine = loads[f * nblk:(f + 1) * nblk]
        mine[0].wait()
        mine[1].wait()

        def build(i, _, f=f):
            for q in range(8):
                at = pl.multiple_of(i * 64 + q * 8, 8)
                gsend[f, pl.ds(at, 8), :] = jnp.where(lane < 64, raw[f, 0, pl.ds(halo + at, 8), :],
                                                      raw[f, nblk - 1, pl.ds(halo + at, 8), :])
            return 0
        lax.fori_loop(0, rows // 64, build, 0)
        cols_in = [
            remote(gsend.at[f], raw.at[f, nblk, pl.ds(halo, rows), :], col_sems.at[f], me_row, other),
            remote(gsend.at[f, pl.ds(0, halo), :], raw.at[f, nblk, pl.ds(halo + rows, halo), :],
                   diag_sems.at[f, 0], up, other),
            remote(gsend.at[f, pl.ds(rows - halo, halo), :], raw.at[f, nblk, pl.ds(0, halo), :],
                   diag_sems.at[f, 1], down, other)]
        for cp in mine[2:]:
            cp.wait()
        rows_in = [
            remote(raw.at[f, pl.ds(0, nblk), pl.ds(halo, halo), :],
                   raw.at[f, pl.ds(0, nblk), pl.ds(halo + rows, halo), :], row_sems.at[f, 0], up, me_col),
            remote(raw.at[f, pl.ds(0, nblk), pl.ds(rows, halo), :],
                   raw.at[f, pl.ds(0, nblk), pl.ds(0, halo), :], row_sems.at[f, 1], down, me_col)]
        halos.append((rows_in, cols_in))

    w = lambda i, j: w_ref[i, j:j + 1, :]
    for k, row in enumerate((0.25 * (w(0, 0) + w(0, 2)), 0.25 * (w(0, 2) - w(0, 0)), 0.5 * w(0, 1),
                              0.5 * w(1, 0), 1.5 + 0.5 * w(1, 1))):
        coef[k] = jnp.broadcast_to(row, (128, steps)).T

    groups = R // 16
    spare = R % 16

    def reg(r, c):
        return pl.ds(pl.multiple_of((r * NB + c + 1) * 8, 8), 8)

    def line(r, shift=0):
        return pl.ds(pl.multiple_of((r * NB + 1 + shift) * 8, 8), NC * 8)

    def to_lanes(f, i, n, blocks):
        for b in blocks:
            parts = []
            for q in range(n):
                at = pl.ds(i * 16 + q, 8, stride=R)
                x = raw[0, b, at, :]
                if f == 1:
                    x = x - 0.5 * raw[1, b, at, :]
                parts.append(x * SCALE)
            wide[f, i, pl.ds(b * 128, 128), :8 * n] = jnp.concatenate(parts, axis=0).T

    def to_registers(f, i, n):
        for c in range(NC):
            back = wide[f, i, pl.ds(c, 128, stride=NC), :][:, :8 * n].T
            for q in range(n):
                r = i * 16 + q
                x = back[q * 8:q * 8 + 8, :]
                if f == 1:
                    x = state_b[reg(r, c), :] - x
                states[f][reg(r, c), :] = x
                if c == 0:
                    states[f][reg(r, NC), :] = pltpu.roll(x, 127, 1)
                if c == NC - 1:
                    states[f][reg(r, -1), :] = pltpu.roll(x, 1, 1)

    def over_groups(fn):
        lax.fori_loop(0, groups, lambda i, _: (fn(i, 16), 0)[1], 0)
        if spare:
            fn(groups, spare)

    def convert(f):
        for cp in halos[f][0]:
            cp.wait()
        over_groups(lambda i, n: to_lanes(f, i, n, range(nblk)))
        for cp in halos[f][1]:
            cp.wait()
        over_groups(lambda i, n: to_lanes(f, i, n, (nblk,)))
        over_groups(lambda i, n: to_registers(f, i, n))

    def clear(r, _):
        state_b[line(r), :] = jnp.zeros((NC * 8, 128), jnp.float32)
        return 0
    lax.fori_loop(0, R, clear, 0)
    convert(0)

    def level(t, cur, new):
        alpha, beta, side, mid_s, centre = (coef[k, pl.ds(t, 1), :] for k in range(5))

        def contrib(r):
            left, here, right = cur[line(r, -1), :], cur[line(r), :], cur[line(r, 1), :]
            s, d = left + right, right - left
            e, bd = alpha * s + side * here, beta * d
            return e + bd, mid_s * s + centre * here, e - bd

        def edges(ref, r):
            ref[reg(r, NC), :] = pltpu.roll(ref[reg(r, 0), :], 127, 1)
            ref[reg(r, -1), :] = pltpu.roll(ref[reg(r, NC - 1), :], 1, 1)

        def turn(x, by):
            return jnp.concatenate([pltpu.roll(x[8 * c:8 * c + 8, :], by, 0) for c in range(NC)], axis=0)

        half = R // 2
        part = half // PARTS

        def sweep(first, step, seam_turn, lag):
            fwd, back = (0, 2) if step > 0 else (2, 0)
            here = contrib(first)
            away, acc = here[fwd], turn(contrib(R - 1 - first)[fwd], seam_turn) + here[1]
            for it in range(PARTS):
                for q in range(part):
                    lag(it, q)
                for q in range(part):
                    r = first + step * (it * part + q)
                    nxt = contrib(r + step)
                    new[line(r), :] = (acc + nxt[back]) - new[line(r), :]
                    away, acc = nxt[fwd], away + nxt[1]

        def lag_down(it, q):
            if it == 0:
                edges(cur, half + q)
            else:
                edges(new, (it - 1) * part + q)

        def lag_up(it, q):
            if it == 0:
                edges(new, half - part + q)
            else:
                edges(new, R - it * part + q)
        sweep(0, 1, 1, lag_down)
        sweep(R - 1, -1, 7, lag_up)

    def strided(r, c, s):
        return pl.ds((r * NB + c + 1) * 8 + s, 8, stride=NB * 8)

    def copies(f, slot):
        return [pltpu.make_async_remote_copy(
            src_ref=sbuf.at[slot, d, f], dst_ref=rbuf.at[slot, d, f], send_sem=send_sems.at[slot, d, f],
            recv_sem=recv_sems.at[slot, d, f], device_id={"row": peer, "col": me_col}, device_id_type=MESH)
            for d, peer in enumerate((up, down))]

    def send(f, slot):
        for d, (r0, s) in enumerate(((halo, 0), (R - 2 * halo, 7))):
            for g in range(halo // 8):
                for c in range(NC):
                    sbuf[slot, d, f, g, c] = states[f][strided(r0 + 8 * g, c, s), :]
        for cp in copies(f, slot):
            cp.start()

    def receive(f, slot):
        for d, (r0, s) in enumerate(((R - halo, 7), (0, 0))):
            copies(f, slot)[d].wait()
            for g in range(halo // 8):
                for c in range(NC):
                    states[f][strided(r0 + 8 * g, c, s), :] = rbuf[slot, d, f, g, c]

        def fix(i, _):
            for r0 in (0, R - halo):
                for q in range(8):
                    r = r0 + i * 8 + q
                    states[f][reg(r, NC), :] = pltpu.roll(states[f][reg(r, 0), :], 127, 1)
                    states[f][reg(r, -1), :] = pltpu.roll(states[f][reg(r, NC - 1), :], 1, 1)
            return 0
        lax.fori_loop(0, halo // 8, fix, 0)

    def pair(i, _):
        level(2 * i, state_a, state_b)

        @pl.when(i == 0)
        def _():
            convert(1)
        done = lax.rem(2 * i + 2, halo) == 0
        more = 2 * i + 2 < steps
        slot = lax.rem((2 * i + 2) // halo, 2)

        @pl.when(done & more)
        def _():
            send(1, slot)
        level(2 * i + 1, state_b, state_a)

        @pl.when(done & more)
        def _():
            send(0, slot)
            receive(1, slot)
            receive(0, slot)
        return 0
    lax.fori_loop(0, steps // 2, pair, 0)

    out_groups = (R - 1) // 16
    outs = []
    for f, dst in enumerate((uo_hbm, vo_hbm)):
        def ungroup(i, _, f=f):
            r0 = i * (R - 16) // out_groups
            for c in range(NC):
                parts = []
                for q in range(16):
                    x = state_a[reg(r0 + q, c), :]
                    if f == 1:
                        x = (x - state_b[reg(r0 + q, c), :]) * (2.0 / SCALE)
                    else:
                        x = x * (1.0 / SCALE)
                    parts.append(x)
                wide[f, i, pl.ds(c, 128, stride=NC), :] = jnp.concatenate(parts, axis=0).T
            for b in range(nblk):
                back = wide[f, i, pl.ds(b * 128, 128), :].T
                for q in range(16):
                    raw[f, b, pl.ds(r0 + q, 8, stride=R), :] = back[q * 8:q * 8 + 8, :]
            return 0
        lax.fori_loop(0, out_groups + 1, ungroup, 0)
        for b in range(nblk):
            cp = pltpu.make_async_copy(raw.at[f, b, pl.ds(halo, rows), :], dst.at[:, pl.ds(b * 128, 128)],
                                       out_sem.at[f, b])
            cp.start()
            outs.append(cp)
    for cp in outs:
        cp.wait()


def solution(mesh):
    tile_spec = P(("ens", "row"), "col")

    def local_run(u_tile, v_tile, stencil_w):
        rows, cols = u_tile.shape
        steps = stencil_w.shape[0]
        halo = HALO
        R = (rows + 2 * halo) // 8
        nblk = cols // 128
        f32 = jnp.float32
        dma = pltpu.SemaphoreType.DMA
        return pl.pallas_call(
            functools.partial(kernel, steps, rows, cols, halo),
            out_shape=[jax.ShapeDtypeStruct((rows, cols), f32)] * 2,
            in_specs=[pl.BlockSpec(memory_space=pltpu.VMEM)] + [pl.BlockSpec(memory_space=pl.ANY)] * 2,
            out_specs=[pl.BlockSpec(memory_space=pl.ANY)] * 2,
            scratch_shapes=[
                pltpu.VMEM((2, nblk + 1, 8 * R, 128), f32),
                pltpu.VMEM((2, rows, 128), f32),
                pltpu.VMEM((R * NB * 8, 128), f32),
                pltpu.VMEM((R * NB * 8, 128), f32),
                pltpu.VMEM((5, steps, 128), f32),
                pltpu.VMEM((2, -(-R // 16), 128 * NC, 128), f32),
                pltpu.VMEM((2, 2, 2, halo // 8, NC, 8, 128), f32),
                pltpu.VMEM((2, 2, 2, halo // 8, NC, 8, 128), f32),
                dma((2, nblk)), dma((2, 2)), dma((2, 2, 2)), dma((2, 2, 2)), dma((2, 2, 2)), dma((2, 2, 2)), dma((2, nblk)),
            ],
            compiler_params=pltpu.CompilerParams(collective_id=0, has_side_effects=True,
                                                 vmem_limit_bytes=48 * 1024 * 1024),
        )(stencil_w.transpose(1, 2, 0), u_tile, v_tile)

    return jax.shard_map(local_run, mesh=mesh, in_specs=(tile_spec, tile_spec, P()), out_specs=(tile_spec, tile_spec), check_vma=False)
```

time: 122 us -> 118 us (0.967)
  Pallas kernels: 118 us -> 114 us
    pallas_call x1, Pallas kernels: 118 us -> 114 us  [local_run(): pl.pallas_call(functools.partial(kernel, steps, rows, cols, halo), out_sh...]
    unnamed x3 -> x4, local copies, waits for them, and re-layouts: 3.45 us -> 3.32 us
where the time goes in v3:
time: 118 us
  Pallas kernels  114 us (97%)
  local copies, waits for them, and re-layouts  3.32 us (3%)
    pallas_call x1, Pallas kernels, local_run(): pl.pallas_call(functools.partial(kernel, steps, rows, cols, halo), out_sh...  114 us
    unnamed x4, local copies, waits for them, and re-layouts  3.32 us

profile of v3, /device:TPU:0, one launch (start us, length us, event | category | flops | bytes accessed | tf_op | source)
XLA Modules:
  0.0 118.2 jit_solution(3011802467446196872)
XLA Ops:
  0.6 0.0 copy-start
  0.6 0.7 copy-done
  1.3 114.2 %shard_map.50 = (f32[512,1024]{1,0:T(8,128)S(1)}, f32[512,1024]{1,0:T(8,128)S(1)}) custom-call(f32[3,3,64]{2,1,0:T(4,128)S(1)} %bitcast.1, f32[512,1024]{1,0:T(8,128)} %u_hbm.1, f32[512,1024]{1,0:T(8,128)} %v_hbm.1), custom_call_target="tpu_custom_call" | custom-call | tf_op jit(solution)/shard_map/pallas_call | solution.py:281
  115.5 1.3 %copy.7 = f32[512,1024]{1,0:T(8,128)} copy(f32[512,1024]{1,0:T(8,128)S(1)} %get-tuple-element.4) | data formatting | bytes 4194304
  116.8 1.3 %copy.8 = f32[512,1024]{1,0:T(8,128)} copy(f32[512,1024]{1,0:T(8,128)S(1)} %get-tuple-element.5) | data formatting | bytes 4194304
Async XLA Ops:
  0.6 0.7 copy-start

commit v4 on v3

--- a/solution.py
+++ b/solution.py
@@ -8,7 +8,7 @@
 from jax.sharding import PartitionSpec as P
 
 HALO = 16
-PARTS = 2
+AHEAD = 4
 NC = 9
 NB = 11
 SCALE = 0.125
@@ -90,30 +90,29 @@
     def line(r, shift=0):
         return pl.ds(pl.multiple_of((r * NB + 1 + shift) * 8, 8), NC * 8)
 
+    def in_registers(base, q, c):
+        return pl.ds(pl.multiple_of(base + (q * NB + c + 1) * 8, 8), 8)
+
     def to_lanes(f, i, n, blocks):
+        r0 = i * 16
         for b in blocks:
-            parts = []
-            for q in range(n):
-                at = pl.ds(i * 16 + q, 8, stride=R)
-                x = raw[0, b, at, :]
-                if f == 1:
-                    x = x - 0.5 * raw[1, b, at, :]
-                parts.append(x * SCALE)
-            wide[f, i, pl.ds(b * 128, 128), :8 * n] = jnp.concatenate(parts, axis=0).T
+            x = jnp.concatenate([raw[f, b, pl.ds(r0 + q, 8, stride=R), :] for q in range(n)], axis=0)
+            wide[f, i, pl.ds(b * 128, 128), :8 * n] = (x * (0.5 * SCALE if f else SCALE)).T
 
     def to_registers(f, i, n):
+        base = i * (16 * NB * 8)
         for c in range(NC):
             back = wide[f, i, pl.ds(c, 128, stride=NC), :][:, :8 * n].T
-            for q in range(n):
-                r = i * 16 + q
-                x = back[q * 8:q * 8 + 8, :]
-                if f == 1:
-                    x = state_b[reg(r, c), :] - x
-                states[f][reg(r, c), :] = x
-                if c == 0:
-                    states[f][reg(r, NC), :] = pltpu.roll(x, 127, 1)
-                if c == NC - 1:
-                    states[f][reg(r, -1), :] = pltpu.roll(x, 1, 1)
+            if f == 1:
+                back = jnp.concatenate([state_b[in_registers(base, q, c), :] for q in range(n)], axis=0) + back
+            puts = [(c, back)]
+            if c == 0:
+                puts.append((NC, pltpu.roll(back, 127, 1)))
+            if c == NC - 1:
+                puts.append((-1, pltpu.roll(back, 1, 1)))
+            for to, x in puts:
+                for q in range(n):
+                    states[f][in_registers(base, q, to), :] = x[q * 8:q * 8 + 8, :]
 
     def over_groups(fn):
         lax.fori_loop(0, groups, lambda i, _: (fn(i, 16), 0)[1], 0)
@@ -129,14 +128,16 @@
         over_groups(lambda i, n: to_lanes(f, i, n, (nblk,)))
         over_groups(lambda i, n: to_registers(f, i, n))
 
-    def clear(r, _):
-        state_b[line(r), :] = jnp.zeros((NC * 8, 128), jnp.float32)
+    convert(0)
+
+    def same(r, _):
+        state_b[line(r), :] = state_a[line(r), :]
         return 0
-    lax.fori_loop(0, R, clear, 0)
-    convert(0)
-
-    def level(t, cur, new):
-        alpha, beta, side, mid_s, centre = (coef[k, pl.ds(t, 1), :] for k in range(5))
+    lax.fori_loop(0, R, same, 0)
+
+    def step(t, cur, new):
+        alpha, beta, side, mid_s, centre = (
+            jnp.broadcast_to(coef[k, pl.ds(t, 1), :], (NC * 8, 128)) for k in range(5))
 
         def contrib(r):
             left, here, right = cur[line(r, -1), :], cur[line(r), :], cur[line(r, 1), :]
@@ -144,42 +145,48 @@
             e, bd = alpha * s + side * here, beta * d
             return e + bd, mid_s * s + centre * here, e - bd
 
-        def edges(ref, r):
-            ref[reg(r, NC), :] = pltpu.roll(ref[reg(r, 0), :], 127, 1)
-            ref[reg(r, -1), :] = pltpu.roll(ref[reg(r, NC - 1), :], 1, 1)
-
-        def turn(x, by):
-            return jnp.concatenate([pltpu.roll(x[8 * c:8 * c + 8, :], by, 0) for c in range(NC)], axis=0)
-
-        half = R // 2
-        part = half // PARTS
-
-        def sweep(first, step, seam_turn, lag):
-            fwd, back = (0, 2) if step > 0 else (2, 0)
-            here = contrib(first)
-            away, acc = here[fwd], turn(contrib(R - 1 - first)[fwd], seam_turn) + here[1]
-            for it in range(PARTS):
-                for q in range(part):
-                    lag(it, q)
-                for q in range(part):
-                    r = first + step * (it * part + q)
-                    nxt = contrib(r + step)
-                    new[line(r), :] = (acc + nxt[back]) - new[line(r), :]
-                    away, acc = nxt[fwd], away + nxt[1]
-
-        def lag_down(it, q):
-            if it == 0:
-                edges(cur, half + q)
-            else:
-                edges(new, (it - 1) * part + q)
-
-        def lag_up(it, q):
-            if it == 0:
-                edges(new, half - part + q)
-            else:
-                edges(new, R - it * part + q)
-        sweep(0, 1, 1, lag_down)
-        sweep(R - 1, -1, 7, lag_up)
+        def store(r, x):
+            new[line(r), :] = x - new[line(r), :]
+        return contrib, store, new
+
+    def edges(ref, r):
+        at = lambda c: pl.ds((r * NB + c + 1) * 8, 8)
+        ref[at(NC), :] = pltpu.roll(ref[at(0), :], 127, 1)
+        ref[at(-1), :] = pltpu.roll(ref[at(NC - 1), :], 1, 1)
+
+    def turn(x, by):
+        return jnp.concatenate([pltpu.roll(x[8 * c:8 * c + 8, :], by, 0) for c in range(NC)], axis=0)
+
+    def cross(x, r, to):
+        if (r, to) == (R - 1, 0):
+            return turn(x, 1)
+        return turn(x, 7) if (r, to) == (0, R - 1) else x
+
+    def arc(at, first, count, way, late):
+        contrib, store, new = at
+        fwd, back = (0, 2) if way > 0 else (2, 0)
+        before, r = (first - way) % R, first % R
+        here = contrib(r)
+        away, acc = here[fwd], cross(contrib(before)[fwd], before, r) + here[1]
+        for n in (count // 2, count - count // 2):
+            for ref, row in late:
+                edges(ref, row)
+            late = []
+            for _ in range(n):
+                to = (r + way) % R
+                nxt = contrib(to)
+                store(r, acc + cross(nxt[back], to, r))
+                away, acc = nxt[fwd], cross(away, r, to) + nxt[1]
+                late.append((new, r))
+                r = to
+        return late
+
+    half = R // 2
+
+    def level(t, cur, new):
+        at = step(t, cur, new)
+        late = arc(at, 0, half, 1, [(cur, half + q) for q in range(half - half // 2)])
+        arc(at, R - 1, R - half, -1, late)
 
     def strided(r, c, s):
         return pl.ds((r * NB + c + 1) * 8 + s, 8, stride=NB * 8)
@@ -205,53 +212,62 @@
                 for c in range(NC):
                     states[f][strided(r0 + 8 * g, c, s), :] = rbuf[slot, d, f, g, c]
 
-        def fix(i, _):
-            for r0 in (0, R - halo):
-                for q in range(8):
-                    r = r0 + i * 8 + q
-                    states[f][reg(r, NC), :] = pltpu.roll(states[f][reg(r, 0), :], 127, 1)
-                    states[f][reg(r, -1), :] = pltpu.roll(states[f][reg(r, NC - 1), :], 1, 1)
-            return 0
-        lax.fori_loop(0, halo // 8, fix, 0)
+    def after_exchange(t0, slot):
+        at = [step(t0 + j, states[j % 2], states[1 - j % 2]) for j in range(AHEAD)]
+        late = [(state_a, half + q) for q in range(half - half // 2)]
+        for j in range(AHEAD):
+            late = arc(at[j], halo + 1 + j, R - 2 * halo - 2 - 2 * j, 1, late)
+        receive(1, slot)
+        receive(0, slot)
+        for r in (*range(halo), *range(R - halo, R)):
+            edges(state_a, r)
+        for j in range(AHEAD):
+            late = arc(at[j], R - halo - 1 - j, 2 * halo + 2 + 2 * j, 1, late)
+        for ref, r in late:
+            edges(ref, r)
 
     def pair(i, _):
         level(2 * i, state_a, state_b)
+        nth = (i + 1) * 2 // halo
+        leave = (lax.rem(2 * i + 2, halo) == 0) & (2 * i + 2 < steps)
 
         @pl.when(i == 0)
         def _():
             convert(1)
-        done = lax.rem(2 * i + 2, halo) == 0
-        more = 2 * i + 2 < steps
-        slot = lax.rem((2 * i + 2) // halo, 2)
-
-        @pl.when(done & more)
+
+        @pl.when(leave)
         def _():
-            send(1, slot)
+            send(1, lax.rem(nth, 2))
         level(2 * i + 1, state_b, state_a)
 
-        @pl.when(done & more)
+        @pl.when(leave)
         def _():
-            send(0, slot)
-            receive(1, slot)
-            receive(0, slot)
+            send(0, lax.rem(nth, 2))
         return 0
-    lax.fori_loop(0, steps // 2, pair, 0)
+
+    phases = steps // halo
+
+    def phase(p, _):
+        @pl.when(p > 0)
+        def _():
+            after_exchange(p * halo, lax.rem(p, 2))
+        lax.fori_loop(p * (halo // 2) + (p + phases - 1) // phases * (AHEAD // 2), (p + 1) * (halo // 2), pair, 0)
+        return 0
+    lax.fori_loop(0, phases, phase, 0)
 
     out_groups = (R - 1) // 16
     outs = []
     for f, dst in enumerate((uo_hbm, vo_hbm)):
         def ungroup(i, _, f=f):
             r0 = i * (R - 16) // out_groups
+            base = r0 * (NB * 8)
+
+            def gathered(ref, c):
+                return jnp.concatenate([ref[in_registers(base, q, c), :] for q in range(16)], axis=0)
             for c in range(NC):
-                parts = []
-                for q in range(16):
-                    x = state_a[reg(r0 + q, c), :]
-                    if f == 1:
-                        x = (x - state_b[reg(r0 + q, c), :]) * (2.0 / SCALE)
-                    else:
-                        x = x * (1.0 / SCALE)
-                    parts.append(x)
-                wide[f, i, pl.ds(c, 128, stride=NC), :] = jnp.concatenate(parts, axis=0).T
+                x = gathered(state_a, c)
+                x = x * (1.0 / SCALE) if f == 0 else (x - gathered(state_b, c)) * (2.0 / SCALE)
+                wide[f, i, pl.ds(c, 128, stride=NC), :] = x.T
             for b in range(nblk):
                 back = wide[f, i, pl.ds(b * 128, 128), :].T
                 for q in range(16):

time: 118 us -> 111 us (0.941)
  Pallas kernels: 114 us -> 107 us
    pallas_call x1, Pallas kernels: 114 us -> 107 us  [local_run(): pl.pallas_call(functools.partial(kernel, steps, rows, cols, halo), out_sh...]
where the time goes in v4:
time: 111 us
  Pallas kernels  107 us (96%)
  local copies, waits for them, and re-layouts  3.32 us (3%)
    pallas_call x1, Pallas kernels, local_run(): pl.pallas_call(functools.partial(kernel, steps, rows, cols, halo), out_sh...  107 us
    unnamed x4, local copies, waits for them, and re-layouts  3.32 us

profile of v4, /device:TPU:0, one launch (start us, length us, event | category | flops | bytes accessed | tf_op | source)
XLA Modules:
  0.0 110.9 jit_solution(10566975641274934337)
XLA Ops:
  0.6 0.0 copy-start
  0.6 0.7 copy-done
  1.3 106.9 %shard_map.50 = (f32[512,1024]{1,0:T(8,128)S(1)}, f32[512,1024]{1,0:T(8,128)S(1)}) custom-call(f32[3,3,64]{2,1,0:T(4,128)S(1)} %bitcast.1, f32[512,1024]{1,0:T(8,128)} %u_hbm.1, f32[512,1024]{1,0:T(8,128)} %v_hbm.1), custom_call_target="tpu_custom_call" | custom-call | tf_op jit(solution)/shard_map/pallas_call | solution.py:297
  108.3 1.3 %copy.7 = f32[512,1024]{1,0:T(8,128)} copy(f32[512,1024]{1,0:T(8,128)S(1)} %get-tuple-element.4) | data formatting | bytes 4194304
  109.6 1.3 %copy.8 = f32[512,1024]{1,0:T(8,128)} copy(f32[512,1024]{1,0:T(8,128)S(1)} %get-tuple-element.5) | data formatting | bytes 4194304
Async XLA Ops:
  0.6 0.7 copy-start

commit v5 on v4

--- a/solution.py
+++ b/solution.py
@@ -15,15 +15,18 @@
 MESH = pl.DeviceIdType.MESH
 
 
-def kernel(steps, rows, cols, halo, w_ref, u_hbm, v_hbm, uo_hbm, vo_hbm,
-           raw, gsend, state_a, state_b, coef, wide, sbuf, rbuf,
-           load_sem, col_sems, row_sems, diag_sems, send_sems, recv_sems, out_sem):
+def kernel(steps, rows, cols, halo, w_hbm, u_hbm, v_hbm, state_a, state_b,
+           raw, gsend, w_ref, coef, wide, sbuf, rbuf,
+           load_sem, col_sems, row_sems, diag_sems, send_sems, recv_sems, w_sem):
     R = (rows + 2 * halo) // 8
     nblk = cols // 128
     n_row = lax.axis_size("row")
     me_row, me_col = lax.axis_index("row"), lax.axis_index("col")
     up, down = lax.rem(me_row + n_row - 1, n_row), lax.rem(me_row + 1, n_row)
     other = 1 - me_col
+
+    weights = pltpu.make_async_copy(w_hbm, w_ref, w_sem)
+    weights.start()
 
     loads = []
     for f, src in enumerate((u_hbm, v_hbm)):
@@ -76,6 +79,7 @@
                    raw.at[f, pl.ds(0, nblk), pl.ds(0, halo), :], row_sems.at[f, 1], down, me_col)]
         halos.append((rows_in, cols_in))
 
+    weights.wait()
     w = lambda i, j: w_ref[i, j:j + 1, :]
     for k, row in enumerate((0.25 * (w(0, 0) + w(0, 2)), 0.25 * (w(0, 2) - w(0, 0)), 0.5 * w(0, 1),
                               0.5 * w(1, 0), 1.5 + 0.5 * w(1, 1))):
@@ -255,31 +259,35 @@
         return 0
     lax.fori_loop(0, phases, phase, 0)
 
-    out_groups = (R - 1) // 16
-    outs = []
-    for f, dst in enumerate((uo_hbm, vo_hbm)):
-        def ungroup(i, _, f=f):
-            r0 = i * (R - 16) // out_groups
-            base = r0 * (NB * 8)
-
-            def gathered(ref, c):
-                return jnp.concatenate([ref[in_registers(base, q, c), :] for q in range(16)], axis=0)
+
+def unpack_kernel(halo, a_ref, b_ref, u_hbm, v_hbm, raw, wide, sems):
+    rows, cols = u_hbm.shape
+    R = (rows + 2 * halo) // 8
+    groups = [(r0, min(16, R - r0)) for r0 in range(0, R, 16)]
+    copies = []
+    for f, dst in enumerate((u_hbm, v_hbm)):
+        for g, (r0, n) in enumerate(groups):
             for c in range(NC):
-                x = gathered(state_a, c)
-                x = x * (1.0 / SCALE) if f == 0 else (x - gathered(state_b, c)) * (2.0 / SCALE)
-                wide[f, i, pl.ds(c, 128, stride=NC), :] = x.T
-            for b in range(nblk):
-                back = wide[f, i, pl.ds(b * 128, 128), :].T
-                for q in range(16):
+                parts = []
+                for q in range(n):
+                    at = pl.ds(((r0 + q) * NB + c + 1) * 8, 8)
+                    if f == 0:
+                        x = a_ref[at, :] * (1.0 / SCALE)
+                    else:
+                        x = (a_ref[at, :] - b_ref[at, :]) * (2.0 / SCALE)
+                    parts.append(x)
+                wide[f, g, pl.ds(c, 128, stride=NC), :8 * n] = jnp.concatenate(parts, axis=0).T
+        for b in range(cols // 128):
+            for g, (r0, n) in enumerate(groups):
+                back = wide[f, g, pl.ds(b * 128, 128), :][:, :8 * n].T
+                for q in range(n):
                     raw[f, b, pl.ds(r0 + q, 8, stride=R), :] = back[q * 8:q * 8 + 8, :]
-            return 0
-        lax.fori_loop(0, out_groups + 1, ungroup, 0)
-        for b in range(nblk):
-            cp = pltpu.make_async_copy(raw.at[f, b, pl.ds(halo, rows), :], dst.at[:, pl.ds(b * 128, 128)],
-                                       out_sem.at[f, b])
-            cp.start()
-            outs.append(cp)
-    for cp in outs:
+            copies.append(pltpu.make_async_copy(raw.at[f, b, pl.ds(halo, rows), :], dst.at[:, pl.ds(b * 128, 128)],
+                                                sems.at[f, b]))
+            if len(copies) > 1:
+                copies[-2].start()
+    copies[-1].start()
+    for cp in copies:
         cp.wait()
 
 
@@ -294,24 +302,29 @@
         nblk = cols // 128
         f32 = jnp.float32
         dma = pltpu.SemaphoreType.DMA
-        return pl.pallas_call(
+        raw = pltpu.VMEM((2, nblk + 1, 8 * R, 128), f32)
+        wide = pltpu.VMEM((2, -(-R // 16), 128 * NC, 128), f32)
+        vmem, hbm = pl.BlockSpec(memory_space=pltpu.VMEM), pl.BlockSpec(memory_space=pl.ANY)
+        states = pl.pallas_call(
             functools.partial(kernel, steps, rows, cols, halo),
-            out_shape=[jax.ShapeDtypeStruct((rows, cols), f32)] * 2,
-            in_specs=[pl.BlockSpec(memory_space=pltpu.VMEM)] + [pl.BlockSpec(memory_space=pl.ANY)] * 2,
-            out_specs=[pl.BlockSpec(memory_space=pl.ANY)] * 2,
+            out_shape=[jax.ShapeDtypeStruct((R * NB * 8, 128), f32)] * 2,
+            in_specs=[hbm, hbm, hbm],
+            out_specs=[vmem, vmem],
             scratch_shapes=[
-                pltpu.VMEM((2, nblk + 1, 8 * R, 128), f32),
-                pltpu.VMEM((2, rows, 128), f32),
-                pltpu.VMEM((R * NB * 8, 128), f32),
-                pltpu.VMEM((R * NB * 8, 128), f32),
-                pltpu.VMEM((5, steps, 128), f32),
-                pltpu.VMEM((2, -(-R // 16), 128 * NC, 128), f32),
-                pltpu.VMEM((2, 2, 2, halo // 8, NC, 8, 128), f32),
-                pltpu.VMEM((2, 2, 2, halo // 8, NC, 8, 128), f32),
-                dma((2, nblk)), dma((2, 2)), dma((2, 2, 2)), dma((2, 2, 2)), dma((2, 2, 2)), dma((2, 2, 2)), dma((2, nblk)),
+                raw, pltpu.VMEM((2, rows, 128), f32), pltpu.VMEM((3, 3, steps), f32), pltpu.VMEM((5, steps, 128), f32), wide,
+                pltpu.VMEM((2, 2, 2, halo // 8, NC, 8, 128), f32), pltpu.VMEM((2, 2, 2, halo // 8, NC, 8, 128), f32),
+                dma((2, nblk)), dma((2, 2)), dma((2, 2, 2)), dma((2, 2, 2)), dma((2, 2, 2)), dma((2, 2, 2)), dma,
             ],
             compiler_params=pltpu.CompilerParams(collective_id=0, has_side_effects=True,
-                                                 vmem_limit_bytes=48 * 1024 * 1024),
-        )(stencil_w.transpose(1, 2, 0), u_tile, v_tile)
+                                                 vmem_limit_bytes=44 * 1024 * 1024),
+        )(*(pltpu.with_memory_space_constraint(x, pltpu.HBM) for x in (stencil_w.transpose(1, 2, 0), u_tile, v_tile)))
+        return pl.pallas_call(
+            functools.partial(unpack_kernel, halo),
+            out_shape=[jax.ShapeDtypeStruct((rows, cols), f32)] * 2,
+            in_specs=[vmem, vmem],
+            out_specs=[hbm, hbm],
+            scratch_shapes=[raw, wide, dma((2, nblk))],
+            compiler_params=pltpu.CompilerParams(vmem_limit_bytes=32 * 1024 * 1024),
+        )(*states)
 
     return jax.shard_map(local_run, mesh=mesh, in_specs=(tile_spec, tile_spec, P()), out_specs=(tile_spec, tile_spec), check_vma=False)

time: 111 us -> 107 us (0.964)
  local copies, waits for them, and re-layouts: 3.32 us -> 0 us
    pallas_call x1, Pallas kernels: 107 us -> 102 us  [local_run(): pl.pallas_call(functools.partial(kernel, steps, rows, cols, halo), out_sh...]
    pallas_call x0 -> x1, Pallas kernels: none -> 3.88 us  [local_run(): pl.pallas_call(functools.partial(unpack_kernel, halo), out_shape=[jax.Sha...]
    unnamed x4 -> x0, local copies, waits for them, and re-layouts: 3.32 us -> none
where the time goes in v5:
time: 107 us; the launch traced here: 106 us
  Pallas kernels  106 us (99%)
    pallas_call x1, Pallas kernels, local_run(): pl.pallas_call(functools.partial(kernel, steps, rows, cols, halo), out_sh...  102 us
    pallas_call x1, Pallas kernels, local_run(): pl.pallas_call(functools.partial(unpack_kernel, halo), out_shape=[jax.Sha...  3.88 us

profile of v5, /device:TPU:0, one launch (start us, length us, event | category | flops | bytes accessed | tf_op | source)
XLA Modules:
  0.0 106.4 jit_solution(3207416280838566729)
XLA Ops:
  0.6 101.9 %shard_map.50 = (f32[5984,128]{1,0:T(8,128)S(1)}, f32[5984,128]{1,0:T(8,128)S(1)}) custom-call(f32[3,3,64]{2,1,0:T(4,128)} %bitcast.1, f32[512,1024]{1,0:T(8,128)} %u_hbm.1, f32[512,1024]{1,0:T(8,128)} %v_hbm.1), custom_call_target="tpu_custom_call" | custom-call | tf_op jit(solution)/shard_map/pallas_call | solution.py:308
  102.5 3.9 %shard_map.51 = (f32[512,1024]{1,0:T(8,128)}, f32[512,1024]{1,0:T(8,128)}) custom-call(f32[5984,128]{1,0:T(8,128)S(1)} %get-tuple-element.4.a_ref, f32[5984,128]{1,0:T(8,128)S(1)} %get-tuple-element.5.b_ref), custom_call_target="tpu_custom_call" | custom-call | tf_op jit(solution)/shard_map/pallas_call | solution.py:321

commit v6 on v5

--- a/solution.py
+++ b/solution.py
@@ -8,7 +8,7 @@
 from jax.sharding import PartitionSpec as P
 
 HALO = 16
-AHEAD = 4
+AHEAD = 6
 NC = 9
 NB = 11
 SCALE = 0.125
@@ -43,7 +43,7 @@
     pl.semaphore_wait(barrier, len(peers))
 
     states = (state_a, state_b)
-    lane = lax.broadcasted_iota(jnp.int32, (8, 128), 1)
+    lane = lax.broadcasted_iota(jnp.int32, (64, 128), 1)
 
     def remote(src, dst, sems, r, c):
         cp = pltpu.make_async_remote_copy(src_ref=src, dst_ref=dst, send_sem=sems.at[0], recv_sem=sems.at[1],
@@ -58,10 +58,9 @@
         mine[1].wait()
 
         def build(i, _, f=f):
-            for q in range(8):
-                at = pl.multiple_of(i * 64 + q * 8, 8)
-                gsend[f, pl.ds(at, 8), :] = jnp.where(lane < 64, raw[f, 0, pl.ds(halo + at, 8), :],
-                                                      raw[f, nblk - 1, pl.ds(halo + at, 8), :])
+            at = pl.multiple_of(i * 64, 64)
+            gsend[f, pl.ds(at, 64), :] = jnp.where(lane < 64, raw[f, 0, pl.ds(halo + at, 64), :],
+                                                   raw[f, nblk - 1, pl.ds(halo + at, 64), :])
             return 0
         lax.fori_loop(0, rows // 64, build, 0)
         cols_in = [
@@ -150,7 +149,8 @@
             return e + bd, mid_s * s + centre * here, e - bd
 
         def store(r, x):
-            new[line(r), :] = x - new[line(r), :]
+            at = line(r)
+            new[at, :] = x - new[at, :]
         return contrib, store, new
 
     def edges(ref, r):

time: 107 us -> 104 us (0.972)
  Pallas kernels: 106 us -> 103 us
    pallas_call x1, Pallas kernels: 102 us -> 99.6 us  [local_run(): pl.pallas_call(functools.partial(kernel, steps, rows, cols, halo), out_sh...]
where the time goes in v6:
time: 104 us
  Pallas kernels  103 us (99%)
    pallas_call x1, Pallas kernels, local_run(): pl.pallas_call(functools.partial(kernel, steps, rows, cols, halo), out_sh...  99.6 us
    pallas_call x1, Pallas kernels, local_run(): pl.pallas_call(functools.partial(unpack_kernel, halo), out_shape=[jax.Sha...  3.88 us

profile of v6, /device:TPU:0, one launch (start us, length us, event | category | flops | bytes accessed | tf_op | source)
XLA Modules:
  0.0 104.3 jit_solution(5944497058018157291)
XLA Ops:
  0.6 99.6 %shard_map.50 = (f32[5984,128]{1,0:T(8,128)S(1)}, f32[5984,128]{1,0:T(8,128)S(1)}) custom-call(f32[3,3,64]{2,1,0:T(4,128)} %bitcast.1, f32[512,1024]{1,0:T(8,128)} %u_hbm.1, f32[512,1024]{1,0:T(8,128)} %v_hbm.1), custom_call_target="tpu_custom_call" | custom-call | tf_op jit(solution)/shard_map/pallas_call | solution.py:308
  100.2 3.9 %shard_map.51 = (f32[512,1024]{1,0:T(8,128)}, f32[512,1024]{1,0:T(8,128)}) custom-call(f32[5984,128]{1,0:T(8,128)S(1)} %get-tuple-element.4.a_ref, f32[5984,128]{1,0:T(8,128)S(1)} %get-tuple-element.5.b_ref), custom_call_target="tpu_custom_call" | custom-call | tf_op jit(solution)/shard_map/pallas_call | solution.py:321

commit v7 on v6

--- a/solution.py
+++ b/solution.py
@@ -40,7 +40,6 @@
     peers = [(up, me_col), (down, me_col), (me_row, other), (up, other), (down, other)]
     for r, c in peers:
         pl.semaphore_signal(barrier, inc=1, device_id={"row": r, "col": c}, device_id_type=MESH)
-    pl.semaphore_wait(barrier, len(peers))
 
     states = (state_a, state_b)
     lane = lax.broadcasted_iota(jnp.int32, (64, 128), 1)
@@ -63,6 +62,8 @@
                                                    raw[f, nblk - 1, pl.ds(halo + at, 64), :])
             return 0
         lax.fori_loop(0, rows // 64, build, 0)
+        if f == 0:
+            pl.semaphore_wait(barrier, len(peers))
         cols_in = [
             remote(gsend.at[f], raw.at[f, nblk, pl.ds(halo, rows), :], col_sems.at[f], me_row, other),
             remote(gsend.at[f, pl.ds(0, halo), :], raw.at[f, nblk, pl.ds(halo + rows, halo), :],
@@ -128,7 +129,10 @@
         over_groups(lambda i, n: to_lanes(f, i, n, range(nblk)))
         for cp in halos[f][1]:
             cp.wait()
-        over_groups(lambda i, n: to_lanes(f, i, n, (nblk,)))
+        for i in range(groups):
+            to_lanes(f, i, 16, (nblk,))
+        if spare:
+            to_lanes(f, groups, spare, (nblk,))
         over_groups(lambda i, n: to_registers(f, i, n))
 
     convert(0)
@@ -143,13 +147,13 @@
             jnp.broadcast_to(coef[k, pl.ds(t, 1), :], (NC * 8, 128)) for k in range(5))
 
         def contrib(r):
-            left, here, right = cur[line(r, -1), :], cur[line(r), :], cur[line(r, 1), :]
+            left, here, right = cur[line(r, -1), :], cur[line(r), :], cur[pl.ds((r * NB + 2) * 8, NC * 8), :]
             s, d = left + right, right - left
             e, bd = alpha * s + side * here, beta * d
             return e + bd, mid_s * s + centre * here, e - bd
 
         def store(r, x):
-            at = line(r)
+            at = pl.ds((r * NB + 1) * 8, NC * 8)
             new[at, :] = x - new[at, :]
         return contrib, store, new
 
@@ -172,7 +176,7 @@
         before, r = (first - way) % R, first % R
         here = contrib(r)
         away, acc = here[fwd], cross(contrib(before)[fwd], before, r) + here[1]
-        for n in (count // 2, count - count // 2):
+        for n in (count // 3, count // 3, count - 2 * (count // 3)):
             for ref, row in late:
                 edges(ref, row)
             late = []
@@ -189,7 +193,7 @@
 
     def level(t, cur, new):
         at = step(t, cur, new)
-        late = arc(at, 0, half, 1, [(cur, half + q) for q in range(half - half // 2)])
+        late = arc(at, 0, half, 1, [(cur, half + q) for q in range(half - 2 * (half // 3))])
         arc(at, R - 1, R - half, -1, late)
 
     def strided(r, c, s):
@@ -218,7 +222,7 @@
 
     def after_exchange(t0, slot):
         at = [step(t0 + j, states[j % 2], states[1 - j % 2]) for j in range(AHEAD)]
-        late = [(state_a, half + q) for q in range(half - half // 2)]
+        late = [(state_a, half + q) for q in range(half - 2 * (half // 3))]
         for j in range(AHEAD):
             late = arc(at[j], halo + 1 + j, R - 2 * halo - 2 - 2 * j, 1, late)
         receive(1, slot)

time: 104 us -> 104 us (level)
  no operation moved by 1% of the time
where the time goes in v7:
time: 104 us
  Pallas kernels  103 us (99%)
    pallas_call x1, Pallas kernels, local_run(): pl.pallas_call(functools.partial(kernel, steps, rows, cols, halo), out_sh...  99.1 us
    pallas_call x1, Pallas kernels, local_run(): pl.pallas_call(functools.partial(unpack_kernel, halo), out_shape=[jax.Sha...  3.88 us

profile of v7, /device:TPU:0, one launch (start us, length us, event | category | flops | bytes accessed | tf_op | source)
XLA Modules:
  0.0 103.8 jit_solution(4982305594864556821)
XLA Ops:
  0.6 99.1 %shard_map.50 = (f32[5984,128]{1,0:T(8,128)S(1)}, f32[5984,128]{1,0:T(8,128)S(1)}) custom-call(f32[3,3,64]{2,1,0:T(4,128)} %bitcast.1, f32[512,1024]{1,0:T(8,128)} %u_hbm.1, f32[512,1024]{1,0:T(8,128)} %v_hbm.1), custom_call_target="tpu_custom_call" | custom-call | tf_op jit(solution)/shard_map/pallas_call | solution.py:312
  99.8 3.9 %shard_map.51 = (f32[512,1024]{1,0:T(8,128)}, f32[512,1024]{1,0:T(8,128)}) custom-call(f32[5984,128]{1,0:T(8,128)S(1)} %get-tuple-element.4.a_ref, f32[5984,128]{1,0:T(8,128)S(1)} %get-tuple-element.5.b_ref), custom_call_target="tpu_custom_call" | custom-call | tf_op jit(solution)/shard_map/pallas_call | solution.py:325

commit v8 on v7

--- a/solution.py
+++ b/solution.py
@@ -149,8 +149,8 @@
         def contrib(r):
             left, here, right = cur[line(r, -1), :], cur[line(r), :], cur[pl.ds((r * NB + 2) * 8, NC * 8), :]
             s, d = left + right, right - left
-            e, bd = alpha * s + side * here, beta * d
-            return e + bd, mid_s * s + centre * here, e - bd
+            bd, e = beta * d, side * here + alpha * s
+            return e + bd, centre * here + mid_s * s, e - bd
 
         def store(r, x):
             at = pl.ds((r * NB + 1) * 8, NC * 8)

time: 104 us -> 103 us (level)
  no operation moved by 1% of the time
where the time goes in v8:
time: 103 us
  Pallas kernels  102 us (99%)
    pallas_call x1, Pallas kernels, local_run(): pl.pallas_call(functools.partial(kernel, steps, rows, cols, halo), out_sh...  98.6 us
    pallas_call x1, Pallas kernels, local_run(): pl.pallas_call(functools.partial(unpack_kernel, halo), out_shape=[jax.Sha...  3.88 us

profile of v8, /device:TPU:0, one launch (start us, length us, event | category | flops | bytes accessed | tf_op | source)
XLA Modules:
  0.0 103.3 jit_solution(15674605289757265851)
XLA Ops:
  0.6 98.6 %shard_map.50 = (f32[5984,128]{1,0:T(8,128)S(1)}, f32[5984,128]{1,0:T(8,128)S(1)}) custom-call(f32[3,3,64]{2,1,0:T(4,128)} %bitcast.1, f32[512,1024]{1,0:T(8,128)} %u_hbm.1, f32[512,1024]{1,0:T(8,128)} %v_hbm.1), custom_call_target="tpu_custom_call" | custom-call | tf_op jit(solution)/shard_map/pallas_call | solution.py:312
  99.2 3.9 %shard_map.51 = (f32[512,1024]{1,0:T(8,128)}, f32[512,1024]{1,0:T(8,128)}) custom-call(f32[5984,128]{1,0:T(8,128)S(1)} %get-tuple-element.4.a_ref, f32[5984,128]{1,0:T(8,128)S(1)} %get-tuple-element.5.b_ref), custom_call_target="tpu_custom_call" | custom-call | tf_op jit(solution)/shard_map/pallas_call | solution.py:325

commit v9 on v8

--- a/solution.py
+++ b/solution.py
@@ -176,7 +176,7 @@
         before, r = (first - way) % R, first % R
         here = contrib(r)
         away, acc = here[fwd], cross(contrib(before)[fwd], before, r) + here[1]
-        for n in (count // 3, count // 3, count - 2 * (count // 3)):
+        for n in (*[count // 4] * 3, count - 3 * (count // 4)):
             for ref, row in late:
                 edges(ref, row)
             late = []
@@ -193,7 +193,7 @@
 
     def level(t, cur, new):
         at = step(t, cur, new)
-        late = arc(at, 0, half, 1, [(cur, half + q) for q in range(half - 2 * (half // 3))])
+        late = arc(at, 0, half, 1, [(cur, half + q) for q in range(half - 3 * (half // 4))])
         arc(at, R - 1, R - half, -1, late)
 
     def strided(r, c, s):
@@ -222,7 +222,7 @@
 
     def after_exchange(t0, slot):
         at = [step(t0 + j, states[j % 2], states[1 - j % 2]) for j in range(AHEAD)]
-        late = [(state_a, half + q) for q in range(half - 2 * (half // 3))]
+        late = [(state_a, half + q) for q in range(half - 3 * (half // 4))]
         for j in range(AHEAD):
             late = arc(at[j], halo + 1 + j, R - 2 * halo - 2 - 2 * j, 1, late)
         receive(1, slot)

time: 103 us -> 103 us (level)
  no operation moved by 1% of the time
where the time goes in v9:
time: 103 us
  Pallas kernels  102 us (99%)
    pallas_call x1, Pallas kernels, local_run(): pl.pallas_call(functools.partial(kernel, steps, rows, cols, halo), out_sh...  98.5 us
    pallas_call x1, Pallas kernels, local_run(): pl.pallas_call(functools.partial(unpack_kernel, halo), out_shape=[jax.Sha...  3.88 us

profile of v9, /device:TPU:0, one launch (start us, length us, event | category | flops | bytes accessed | tf_op | source)
XLA Modules:
  0.0 103.2 jit_solution(14543147963435143866)
XLA Ops:
  0.6 98.5 %shard_map.50 = (f32[5984,128]{1,0:T(8,128)S(1)}, f32[5984,128]{1,0:T(8,128)S(1)}) custom-call(f32[3,3,64]{2,1,0:T(4,128)} %bitcast.1, f32[512,1024]{1,0:T(8,128)} %u_hbm.1, f32[512,1024]{1,0:T(8,128)} %v_hbm.1), custom_call_target="tpu_custom_call" | custom-call | tf_op jit(solution)/shard_map/pallas_call | solution.py:312
  99.2 3.9 %shard_map.51 = (f32[512,1024]{1,0:T(8,128)}, f32[512,1024]{1,0:T(8,128)}) custom-call(f32[5984,128]{1,0:T(8,128)S(1)} %get-tuple-element.4.a_ref, f32[5984,128]{1,0:T(8,128)S(1)} %get-tuple-element.5.b_ref), custom_call_target="tpu_custom_call" | custom-call | tf_op jit(solution)/shard_map/pallas_call | solution.py:325
